TPU v7x, 32 devices: a whole 2x2x4 slice. The times are simulated.
32 devices in a mesh: ga: 8 (over z, x), band: 4 (over y, core).
Axes of the slice: x: 2, y: 2, z: 4, core: 2. Of those that a mesh axis runs over, the one named last changes fastest.
Arguments:
- coeffs: bfloat16 [2, 512, 40960], P(None, ('ga', 'band')), may hold values from -6 to 6
- projectors: bfloat16 [1280, 2, 40960], P(None, None, 'ga'), may hold values from -0.01953125 to 0.01953125
- block_coupling: float32 [1280, 18], replicated, may hold values from -12 to 12
- atom_counts: int32 [160], replicated, may hold values from 4 to 18, as said below
- wave_counts: int32 [8], P('ga'), may hold values from 3840 to 5120
Outputs:
- applied: bfloat16 [2, 512, 40960], P(None, ('ga', 'band'))
- band_energy: float32 [512], P(('ga', 'band'))
- total_energy: float32 [], replicated
Inputs may be any that keep to these rules, and one draw needn't show every extreme that they name: `atom_counts`: each atom has 4, 8 or 18 projectors, the counts sum to 1280 and the largest is 18.
All inputs are finite; a program needn't handle non-finite values.
Results may differ from a plain program's by a relative error of at most 0.013.
Values may be sent and summed in bfloat16 or wider, within the bound.
A program may use at most 128 MiB of HBM per device.

v0:
```python
import math
import jax
import jax.numpy as jnp
from jax import lax
from jax.sharding import PartitionSpec as P


def block_tables(atom_counts, row_ids):
    atom_ends = jnp.cumsum(atom_counts)
    atom_starts = atom_ends - atom_counts
    inside = (atom_starts[None, :] <= row_ids[:, None]) & (atom_ends[None, :] > row_ids[:, None])
    block_first = jnp.sum(jnp.where(inside, atom_starts[None, :], 0), axis=1)
    block_length = jnp.sum(jnp.where(inside, atom_counts[None, :], 0), axis=1)
    return (block_first, block_length)


def coupling_matrix(block_first, block_length, coupling_rows, column_count):
    column_ids = lax.iota(jnp.int32, column_count)
    offsets = column_ids[None, :] - block_first[:, None]
    matrix = jnp.zeros((coupling_rows.shape[0], column_count), jnp.float32)
    for offset in range(coupling_rows.shape[1]):
        hit = (offsets == offset) & (offset < block_length[:, None])
        matrix = jnp.where(hit, coupling_rows[:, offset : offset + 1], matrix)
    return matrix


def shards(coeffs, projectors, block_coupling, atom_counts, wave_counts):
    moved_bands = lax.all_to_all(coeffs, "ga", split_axis=2, concat_axis=1, tiled=True)
    own_bands = coeffs.shape[1]
    group_bands = moved_bands.shape[1]
    wave_slots = projectors.shape[2]
    proj_total_rows = projectors.shape[0]
    in_sphere = (lax.iota(jnp.int32, wave_slots) < wave_counts[0]).astype(jnp.float32)
    masked = moved_bands * in_sphere.astype(jnp.bfloat16)
    real_part = masked[0]
    imag_part = masked[1]
    stacked = jnp.concatenate(
        [jnp.concatenate([real_part, imag_part], 1), jnp.concatenate([imag_part, -real_part], 1)], 0
    )
    flat_beta = projectors.reshape(proj_total_rows, 2 * wave_slots)
    contract_last = (((1,), (1,)), ((), ()))
    contract_first = (((0,), (0,)), ((), ()))
    ga_index = lax.axis_index("ga")
    local_terms = lax.dot_general(
        flat_beta, stacked, contract_last, preferred_element_type=jnp.float32
    )
    projections = lax.psum(local_terms, "ga")
    block_first, block_length = block_tables(atom_counts, lax.iota(jnp.int32, proj_total_rows))
    matrix = coupling_matrix(block_first, block_length, block_coupling, proj_total_rows)
    coupled = jnp.dot(
        matrix, projections, precision=lax.Precision.HIGHEST, preferred_element_type=jnp.float32
    )
    energy_terms = jnp.sum(projections * coupled, axis=0)
    group_energy = (energy_terms[:group_bands] + energy_terms[group_bands:]) / proj_total_rows
    band_energy = lax.dynamic_slice_in_dim(group_energy, ga_index * own_bands, own_bands, 0)
    total_energy = lax.psum(jnp.sum(group_energy), "band")
    products = lax.dot_general(
        coupled.astype(jnp.bfloat16), flat_beta, contract_first, preferred_element_type=jnp.float32
    )
    band_total = own_bands * lax.axis_size("ga") * lax.axis_size("band")
    total_energy = total_energy / math.sqrt(band_total)
    real_out = products[:group_bands, :wave_slots] - products[group_bands:, wave_slots:]
    imag_out = products[:group_bands, wave_slots:] + products[group_bands:, :wave_slots]
    result = (jnp.stack([real_out, imag_out]) * in_sphere).astype(jnp.bfloat16)
    applied = lax.all_to_all(result, "ga", split_axis=1, concat_axis=2, tiled=True)
    return (applied, band_energy, total_energy)


def solution(mesh):
    placed = (P(None, ("ga", "band"), None), P(None, None, "ga"), P(), P(), P("ga"))
    return jax.shard_map(
        shards,
        mesh=mesh,
        in_specs=placed,
        out_specs=(P(None, ("ga", "band"), None), P(("ga", "band")), P()),
        check_vma=False,
    )
```

profile of v0, /device:TPU:0, one launch (start us, length us, event | category | flops | bytes accessed | tf_op | source)
XLA Modules:
  0.0 439.4 jit_solution(13984395675737779399)
XLA Ops:
  7.2 38.0 %copy.21 = bf16[2,16,40960]{1,0,2:T(2,128)(2,1)} copy(bf16[2,16,40960]{2,1,0:T(8,128)(2,1)} %param.5) | data formatting | bytes 5242880 | tf_op args[0]
  45.1 24.1 %reshape.129 = bf16[8,2,81920]{2,1,0:T(2,128)(2,1)} reshape(bf16[40960,2,16]{2,1,0:T(2,128)(2,1)} %bitcast.40) | data formatting | bytes 5242880
  69.2 7.3 %all-to-all-start = ((bf16[8,2,81920]{2,1,0:T(2,128)(2,1)}), bf16[8,2,81920]{2,1,0:T(2,128)(2,1)S(1)}, u32[]{:S(2)}, u32[]{:S(2)}) async-start(bf16[8,2,81920]{2,1,0:T(2,128)(2,1)} %reshape.129), calls=%async_computation | async-start | bytes 5242880 | tf_op jit(solution)/shard_map/all_to_all | solution.py:28
  76.5 0.4 all-reduce.3.cloned.1.call-start
  77.6 23.8 %copy.29 = bf16[160,8,2,5120]{3,1,2,0:T(8,128)(2,1)} copy(bf16[160,8,2,5120]{3,2,1,0:T(2,128)(2,1)} %bitcast.41) | data formatting | bytes 52428800
  101.3 34.6 %all-to-all-done = bf16[8,2,81920]{2,1,0:T(2,128)(2,1)S(1)} async-done(((bf16[8,2,81920]{2,1,0:T(2,128)(2,1)}), bf16[8,2,81920]{2,1,0:T(2,128)(2,1)S(1)}, u32[]{:S(2)}, u32[]{:S(2)}) %all-to-all-start) | async-done | bytes 2621472 | tf_op jit(solution)/shard_map/all_to_all | solution.py:28
  136.0 17.1 %reshape.130 = bf16[40960,2,16]{2,1,0:T(2,128)(2,1)} reshape(bf16[8,2,81920]{2,1,0:T(2,128)(2,1)S(1)} %all-to-all-done) | data formatting | bytes 5242880
  153.0 37.5 %copy.28 = bf16[2,16,8,5120]{3,1,2,0:T(8,128)(2,1)S(1)} copy(bf16[2,16,8,5120]{1,0,3,2:T(2,128)(2,1)} %bitcast.39) | data formatting | bytes 5242880 | tf_op jit(solution)/shard_map/all_to_all | solution.py:28
  190.5 0.3 bitcast_multiply_fusion
  190.9 0.2 slice_bitcast_fusion.1
  191.1 0.1 fusion.168
  191.2 0.0 copy-start.1
  191.2 0.0 copy-start
  191.2 28.8 %fusion.138 = f32[1280,256]{0,1:T(8,128)} fusion(bf16[1280,10240]{1,0:T(8,128)(2,1)} %bitcast.37, bf16[128,5120]{1,0:T(8,128)(2,1)S(1)} %fusion.168, bf16[128,5120]{1,0:T(8,128)(2,1)S(1)} %get-tuple-element.28, bf16[128,5120]{1,0:T(8,128)(2,1)S(1)} %get-tuple-element.27), kind=kOutput, calls=%fused_computation.122 | convolution fusion | flops 6731857920 | bytes 31457280 | tf_op jit(solution)/shard_map/dot_general | solution.py:44
  220.0 0.0 all-reduce.3.cloned.1.call-update
  220.1 0.0 copy-done.1
  220.1 0.3 reduce-window.9
  220.4 0.1 slice.88
  220.5 0.1 slice_reduce_fusion.18
  220.6 0.0 copy-done
  220.6 0.2 slice_reduce_fusion.17
  220.9 0.1 add_bitcast_fusion
  220.9 0.3 select_reduce_fusion
  221.3 81.6 %all-reduce.3.cloned.1.call-done = f32[1280,256]{0,1:T(8,128)} async-done(((f32[1280,256]{0,1:T(8,128)}), f32[1280,256]{0,1:T(8,128)}) %all-reduce.3.cloned.1.call-update) | async-done | bytes 1310736 | tf_op jit(solution)/shard_map/psum | solution.py:47
  303.0 39.1 %fusion = f32[1280,256]{1,0:T(8,128)} fusion(f32[1280,256]{0,1:T(8,128)} %all-reduce.3.cloned.1.call-done, f32[1280]{0:T(1024)S(1)} %get-tuple-element.19, f32[1280]{0:T(1024)S(1)} %get-tuple-element.20, f32[1280]{0:T(1024)S(1)} %get-tuple-element.4, f32[1280]{0:T(1024)S(1)} %get-tuple-element.5, f32[1280]{0:T(1024)S(1)} %get-tuple-element.6, ...), kind=kOutput, calls=%fused_computation | convolution fusion | flops 5123276800 | bytes 2741760 | tf_op jit(solution)/shard_map/dot_general | solution.py:50
  342.1 13.0 %fusion.144 = f32[256,10240]{1,0:T(8,128)S(1)} fusion(bf16[1280,10240]{1,0:T(8,128)(2,1)} %bitcast.38, f32[1280,256]{1,0:T(8,128)} %fusion), kind=kOutput, calls=%fused_computation.136 | convolution fusion | flops 6711214080 | bytes 38010880 | tf_op jit(solution)/shard_map/dot_general | solution.py:57
  355.1 0.8 fusion.142
  355.9 0.5 fusion.81
  356.4 4.2 copy.24
  360.6 3.7 all-to-all-start.1
  364.2 2.8 copy.26
  367.0 1.9 multiply_reduce_fusion
  368.9 0.6 fusion.169
  369.5 7.3 %psum.15 = f32[]{:T(128)} all-reduce(f32[]{:T(128)} %get-tuple-element.23), channel_id=1, replica_groups=mesh['ga'=8,'band'=4] {'band'}, use_global_device_ids=true, to_apply=%region_7.8 | all-reduce | flops 1 | bytes 8 | tf_op jit(solution)/shard_map/psum | solution.py:56
  376.9 0.6 dynamic_slice.3
  378.1 45.7 %all-to-all-done.1 = bf16[2,128,5120]{2,0,1:T(2,128)(2,1)S(1)} async-done(((bf16[2,128,5120]{2,0,1:T(2,128)(2,1)}), bf16[2,128,5120]{2,0,1:T(2,128)(2,1)S(1)}, u32[]{:S(2)}, u32[]{:S(2)}) %all-to-all-start.1) | async-done | bytes 2621472 | tf_op jit(solution)/shard_map/all_to_all | solution.py:65
  423.8 2.9 copy.25
  426.7 4.5 %all_to_all.33 = bf16[2,16,40960]{2,1,0:T(8,128)(2,1)} reshape(bf16[2,16,8,5120]{3,2,1,0:T(8,128)(2,1)} %copy.25) | data formatting | bytes 5242880 | tf_op jit(solution)/shard_map/all_to_all | solution.py:65
  (5 shorter events, 0.1 us)
Async XLA Ops:
  69.2 66.8 %all-to-all-start = ((bf16[8,2,81920]{2,1,0:T(2,128)(2,1)}), bf16[8,2,81920]{2,1,0:T(2,128)(2,1)S(1)}, u32[]{:S(2)}, u32[]{:S(2)}) async-start(bf16[8,2,81920]{2,1,0:T(2,128)(2,1)} %reshape.129), calls=%async_computation | async-start | bytes 5242880 | tf_op jit(solution)/shard_map/all_to_all | solution.py:28
  76.5 226.5 %all-reduce.3.cloned.1.call-start = ((), (), s32[]{:S(2)}) async-start(), calls=%async_computation.2 | async-start | bytes 2621440 | tf_op jit(solution)/shard_map/psum | solution.py:47
  191.2 28.9 %copy-start.1 = (s32[160]{0:T(256)S(1)}, s32[160]{0:T(256)}, u32[]{:S(2)}) copy-start(s32[160]{0:T(256)} %param.8) | copy-start | bytes 1924
  191.2 29.4 %copy-start = (f32[1280,18]{0,1:T(8,128)S(1)}, f32[1280,18]{0,1:T(8,128)}, u32[]{:S(2)}) copy-start(f32[1280,18]{0,1:T(8,128)} %param.7) | copy-start | bytes 276484
  360.6 63.2 %all-to-all-start.1 = ((bf16[2,128,5120]{2,0,1:T(2,128)(2,1)}), bf16[2,128,5120]{2,0,1:T(2,128)(2,1)S(1)}, u32[]{:S(2)}, u32[]{:S(2)}) async-start(bf16[2,128,5120]{2,0,1:T(2,128)(2,1)} %copy.24), calls=%async_computation.1 | async-start | bytes 5242880 | tf_op jit(solution)/shard_map/all_to_all | solution.py:65
Sparse Core Ops, SparseCore 0:
  220.2 82.7 all-reduce.2
where the time goes:
time: 447 us; the launch traced here: 439 us
  waiting for transfers between devices  162 us (36%)
  local copies, waits for them, and re-layouts  156 us (35%)
  matrix products  81 us (18%)
  between operations  16.8 us (4%)
  starting transfers between devices  11.4 us (3%)
  blocking collectives  7.33 us (2%)
  other arithmetic  4.94 us (1%)
    unnamed x8, local copies, waits for them, and re-layouts  103 us
    psum x1, waiting for transfers between devices, shards(): projections = lax.psum(local_terms, 'ga')  81.6 us
    all_to_all x1, waiting for transfers between devices, shards(): lax.all_to_all(result, 'ga', split_axis=1, concat_axis=2, tiled=True)  45.7 us
    dot_general x1, matrix products, shards(): jnp.dot(matrix, projections, precision=lax.Precision.HIGHEST, preferred_e...  39.1 us
    all_to_all x1, local copies, waits for them, and re-layouts, shards(): lax.all_to_all(coeffs, 'ga', split_axis=2, concat_axis=1, tiled=True)  37.5 us
    all_to_all x1, waiting for transfers between devices, shards(): lax.all_to_all(coeffs, 'ga', split_axis=2, concat_axis=1, tiled=True)  34.6 us
    dot_general x1, matrix products, shards(): lax.dot_general(flat_beta, stacked, contract_last, preferred_element_type...  28.8 us
    dot_general x1, matrix products, shards(): lax.dot_general(coupled.astype(jnp.bfloat16), flat_beta, contract_first,...  13 us
  transfers between devices with their start and end apart: 3, of which 3 were waited for; matrix products, arithmetic and copies ran while one was open for 7% of the time, Pallas kernels for 0%

commit v1 on v0

--- a/solution.py
+++ b/solution.py
@@ -25,7 +25,10 @@
 
 
 def shards(coeffs, projectors, block_coupling, atom_counts, wave_counts):
-    moved_bands = lax.all_to_all(coeffs, "ga", split_axis=2, concat_axis=1, tiled=True)
+    moved_bands = jnp.concatenate(
+        lax.all_to_all(jnp.stack(jnp.split(coeffs, lax.axis_size("ga"), axis=2)), "ga", 0, 0),
+        axis=1,
+    )
     own_bands = coeffs.shape[1]
     group_bands = moved_bands.shape[1]
     wave_slots = projectors.shape[2]

time: 447 us -> 328 us (0.73); the launches traced: 439 us -> 327 us
  local copies, waits for them, and re-layouts: 156 us -> 53.3 us
  matrix products: 81 us -> 71.2 us
    unnamed x8 -> x12, local copies, waits for them, and re-layouts: 103 us -> 35.8 us
    all_to_all x1, local copies, waits for them, and re-layouts: 37.5 us -> 0.23 us  [shards(): lax.all_to_all(jnp.stack(jnp.split(coeffs, lax.axis_size('ga'), axis=2)),...]
    dot_general x1, matrix products: 39.1 us -> 29.3 us  [shards(): jnp.dot(matrix, projections, precision=lax.Precision.HIGHEST, preferred_e...]
  transfers between devices with their start and end apart: 3 -> 3, of which waited for: 3 -> 3; matrix products, arithmetic and copies ran while one was open for 7% -> 9% of each run, Pallas kernels for 0% -> 0%
where the time goes in v1:
time: 328 us; the launch traced here: 327 us
  waiting for transfers between devices  162 us (49%)
  matrix products  71.2 us (22%)
  local copies, waits for them, and re-layouts  53.3 us (16%)
  between operations  16.6 us (5%)
  starting transfers between devices  11 us (3%)
  blocking collectives  7.33 us (2%)
  other arithmetic  4.95 us (2%)
    psum x1, waiting for transfers between devices, shards(): projections = lax.psum(local_terms, 'ga')  81.6 us
    all_to_all x1, waiting for transfers between devices, shards(): lax.all_to_all(result, 'ga', split_axis=1, concat_axis=2, tiled=True)  45.7 us
    unnamed x12, local copies, waits for them, and re-layouts  35.8 us
    all_to_all x1, waiting for transfers between devices, shards(): lax.all_to_all(jnp.stack(jnp.split(coeffs, lax.axis_size('ga'), axis=2)),...  35 us
    dot_general x1, matrix products, shards(): jnp.dot(matrix, projections, precision=lax.Precision.HIGHEST, preferred_e...  29.3 us
    dot_general x1, matrix products, shards(): lax.dot_general(flat_beta, stacked, contract_last, preferred_element_type...  28.8 us
    dot_general x1, matrix products, shards(): lax.dot_general(coupled.astype(jnp.bfloat16), flat_beta, contract_first,...  13 us
    all_to_all x2, local copies, waits for them, and re-layouts, shards(): lax.all_to_all(result, 'ga', split_axis=1, concat_axis=2, tiled=True)  7.43 us
  transfers between devices with their start and end apart: 3, of which 3 were waited for; matrix products, arithmetic and copies ran while one was open for 9% of the time, Pallas kernels for 0%

profile of v1, /device:TPU:0, one launch (start us, length us, event | category | flops | bytes accessed | tf_op | source)
XLA Modules:
  0.0 326.7 jit_solution(9085515628055994238)
XLA Ops:
  7.2 1.7 bitcast_dynamic-update-slice_fusion.7
  8.9 1.7 bitcast_dynamic-update-slice_fusion.6
  10.6 1.7 bitcast_dynamic-update-slice_fusion.5
  12.3 1.7 bitcast_dynamic-update-slice_fusion.4
  14.0 1.7 bitcast_dynamic-update-slice_fusion.3
  15.8 1.7 bitcast_dynamic-update-slice_fusion.2
  17.5 1.7 bitcast_dynamic-update-slice_fusion.1
  19.2 1.7 bitcast_dynamic-update-slice_fusion
  20.9 7.3 %all-to-all-start = ((bf16[8,2,16,5120]{3,2,1,0:T(8,128)(2,1)}), bf16[8,2,16,5120]{3,2,1,0:T(8,128)(2,1)S(1)}, u32[]{:S(2)}, u32[]{:S(2)}) async-start(bf16[8,2,16,5120]{3,2,1,0:T(8,128)(2,1)} %bitcast_dynamic-update-slice_fusion), calls=%async_computation | async-start | bytes 5242880 | tf_op jit(solution)/shard_map/all_to_all | solution.py:29
  28.2 0.0 all-reduce.3.cloned.1.call-start
  28.9 23.8 %copy.20 = bf16[160,8,2,5120]{3,1,2,0:T(8,128)(2,1)} copy(bf16[160,8,2,5120]{3,2,1,0:T(2,128)(2,1)} %bitcast.52) | data formatting | bytes 52428800
  52.6 35.0 %all-to-all-done = bf16[8,2,16,5120]{3,2,1,0:T(8,128)(2,1)S(1)} async-done(((bf16[8,2,16,5120]{3,2,1,0:T(8,128)(2,1)}), bf16[8,2,16,5120]{3,2,1,0:T(8,128)(2,1)S(1)}, u32[]{:S(2)}, u32[]{:S(2)}) %all-to-all-start) | async-done | bytes 2621472 | tf_op jit(solution)/shard_map/all_to_all | solution.py:29
  87.7 0.2 copy.16
  87.9 0.3 bitcast_multiply_fusion
  88.2 0.2 slice_bitcast_fusion.1
  88.4 0.1 fusion.168
  88.5 0.0 copy-start.1
  88.5 0.0 copy-start
  88.5 28.8 %fusion.138 = f32[1280,256]{0,1:T(8,128)} fusion(bf16[1280,10240]{1,0:T(8,128)(2,1)} %bitcast.50, bf16[128,5120]{1,0:T(8,128)(2,1)S(1)} %fusion.168, bf16[128,5120]{1,0:T(8,128)(2,1)S(1)} %get-tuple-element.28, bf16[128,5120]{1,0:T(8,128)(2,1)S(1)} %get-tuple-element.27), kind=kOutput, calls=%fused_computation.122 | convolution fusion | flops 6731857920 | bytes 31457280 | tf_op jit(solution)/shard_map/dot_general | solution.py:47
  117.4 0.0 all-reduce.3.cloned.1.call-update
  117.4 0.0 copy-done.1
  117.4 0.3 reduce-window.9
  117.7 0.1 slice.88
  117.8 0.1 slice_reduce_fusion.18
  118.0 0.0 copy-done
  118.0 0.2 slice_reduce_fusion.17
  118.2 0.1 add_bitcast_fusion
  118.3 0.3 select_reduce_fusion
  118.7 81.6 %all-reduce.3.cloned.1.call-done = f32[1280,256]{0,1:T(8,128)} async-done(((f32[1280,256]{0,1:T(8,128)}), f32[1280,256]{0,1:T(8,128)}) %all-reduce.3.cloned.1.call-update) | async-done | bytes 1310736 | tf_op jit(solution)/shard_map/psum | solution.py:50
  200.3 29.3 %fusion = f32[1280,256]{1,0:T(8,128)} fusion(f32[1280,256]{0,1:T(8,128)} %all-reduce.3.cloned.1.call-done, f32[1280]{0:T(1024)S(1)} %get-tuple-element.19, f32[1280]{0:T(1024)S(1)} %get-tuple-element.20, f32[1280]{0:T(1024)S(1)} %get-tuple-element.4, f32[1280]{0:T(1024)S(1)} %get-tuple-element.5, f32[1280]{0:T(1024)S(1)} %get-tuple-element.6, ...), kind=kOutput, calls=%fused_computation | convolution fusion | flops 5123276800 | bytes 2741760 | tf_op jit(solution)/shard_map/dot_general | solution.py:53
  229.6 13.0 %fusion.144 = f32[256,10240]{1,0:T(8,128)S(1)} fusion(bf16[1280,10240]{1,0:T(8,128)(2,1)} %bitcast.51, f32[1280,256]{1,0:T(8,128)} %fusion), kind=kOutput, calls=%fused_computation.136 | convolution fusion | flops 6711214080 | bytes 38010880 | tf_op jit(solution)/shard_map/dot_general | solution.py:60
  242.7 0.8 fusion.142
  243.4 0.5 fusion.81
  243.9 4.2 %copy.17 = bf16[2,128,5120]{2,0,1:T(2,128)(2,1)} copy(bf16[2,128,5120]{2,1,0:T(8,128)(2,1)S(1)} %fusion.81) | data formatting | bytes 5242880 | tf_op jit(solution)/shard_map/convert_element_type | solution.py:67
  248.1 3.7 %all-to-all-start.1 = ((bf16[2,128,5120]{2,0,1:T(2,128)(2,1)}), bf16[2,128,5120]{2,0,1:T(2,128)(2,1)S(1)}, u32[]{:S(2)}, u32[]{:S(2)}) async-start(bf16[2,128,5120]{2,0,1:T(2,128)(2,1)} %copy.17), calls=%async_computation.1 | async-start | bytes 5242880 | tf_op jit(solution)/shard_map/all_to_all | solution.py:68
  251.8 2.8 copy.19
  254.5 1.9 multiply_reduce_fusion
  256.4 0.6 fusion.169
  257.1 7.3 %psum.15 = f32[]{:T(128)} all-reduce(f32[]{:T(128)} %get-tuple-element.23), channel_id=1, replica_groups=mesh['ga'=8,'band'=4] {'band'}, use_global_device_ids=true, to_apply=%region_7.8 | all-reduce | flops 1 | bytes 8 | tf_op jit(solution)/shard_map/psum | solution.py:59
  264.4 0.6 dynamic_slice.3
  265.6 45.7 %all-to-all-done.1 = bf16[2,128,5120]{2,0,1:T(2,128)(2,1)S(1)} async-done(((bf16[2,128,5120]{2,0,1:T(2,128)(2,1)}), bf16[2,128,5120]{2,0,1:T(2,128)(2,1)S(1)}, u32[]{:S(2)}, u32[]{:S(2)}) %all-to-all-start.1) | async-done | bytes 2621472 | tf_op jit(solution)/shard_map/all_to_all | solution.py:68
  311.3 2.9 copy.18
  314.2 4.5 %all_to_all.20 = bf16[2,16,40960]{2,1,0:T(8,128)(2,1)} reshape(bf16[2,16,8,5120]{3,2,1,0:T(8,128)(2,1)} %copy.18) | data formatting | bytes 5242880 | tf_op jit(solution)/shard_map/all_to_all | solution.py:68
  (6 shorter events, 0.1 us)
Async XLA Ops:
  20.9 66.8 %all-to-all-start = ((bf16[8,2,16,5120]{3,2,1,0:T(8,128)(2,1)}), bf16[8,2,16,5120]{3,2,1,0:T(8,128)(2,1)S(1)}, u32[]{:S(2)}, u32[]{:S(2)}) async-start(bf16[8,2,16,5120]{3,2,1,0:T(8,128)(2,1)} %bitcast_dynamic-update-slice_fusion), calls=%async_computation | async-start | bytes 5242880 | tf_op jit(solution)/shard_map/all_to_all | solution.py:29
  28.2 172.1 %all-reduce.3.cloned.1.call-start = ((), (), s32[]{:S(2)}) async-start(), calls=%async_computation.2 | async-start | bytes 2621440 | tf_op jit(solution)/shard_map/psum | solution.py:50
  88.5 28.9 %copy-start.1 = (s32[160]{0:T(256)S(1)}, s32[160]{0:T(256)}, u32[]{:S(2)}) copy-start(s32[160]{0:T(256)} %param.8) | copy-start | bytes 1924
  88.5 29.4 %copy-start = (f32[1280,18]{0,1:T(8,128)S(1)}, f32[1280,18]{0,1:T(8,128)}, u32[]{:S(2)}) copy-start(f32[1280,18]{0,1:T(8,128)} %param.7) | copy-start | bytes 276484
  248.1 63.2 %all-to-all-start.1 = ((bf16[2,128,5120]{2,0,1:T(2,128)(2,1)}), bf16[2,128,5120]{2,0,1:T(2,128)(2,1)S(1)}, u32[]{:S(2)}, u32[]{:S(2)}) async-start(bf16[2,128,5120]{2,0,1:T(2,128)(2,1)} %copy.17), calls=%async_computation.1 | async-start | bytes 5242880 | tf_op jit(solution)/shard_map/all_to_all | solution.py:68
Sparse Core Ops, SparseCore 0:
  117.5 82.7 all-reduce.2
